TPU v7x, 32 devices: a whole 2x2x4 slice. The times are simulated.
32 devices in a mesh: gx: 8 (over z, x), gy: 4 (over y, core).
Axes of the slice: x: 2, y: 2, z: 4, core: 2. Of those that a mesh axis runs over, the one named last changes fastest.
Arguments:
- mode_fields: float32 [32, 512, 1024], P(None, 'gx', 'gy'), may hold values from -60 to 60, as said below
- conductance: float32 [512, 1024], P('gx', 'gy'), may hold values from 0.5 to 2
- potential: float32 [512, 1024], P('gx', 'gy'), may hold values from 0.25 to 4
Outputs:
- basis_field: float32 [128, 512, 1024], P(None, 'gx', 'gy')
- scaled_factor: float32 [128, 128], replicated
Inputs may be any that keep to these rules, and one draw needn't show every extreme that they name: `mode_fields`: Real-valued mode amplitudes.
All inputs are finite; a program needn't handle non-finite values.
Results may differ from a plain program's by a relative error of at most 0.0003.
Values sent between devices are 32-bit elements; how exact they have to be, the bound alone decides.
A program may use at most 64 MiB of HBM per device.

v0:
```python
import jax
import jax.numpy as jnp
from jax import lax
from jax.sharding import PartitionSpec as P


def padded_2(value, sides, width):
    for axis, dim in sides:
        peers, length = (lax.axis_size(axis), value.shape[dim])
        up = [(i, (i + 1) % peers) for i in range(peers - 1)]
        down = [(j, i) for i, j in up]
        last = lax.slice_in_dim(value, length - width, length, axis=dim)
        first = lax.slice_in_dim(value, 0, width, axis=dim)
        before = lax.ppermute(last, axis, up)
        after = lax.ppermute(first, axis, down)
        value = jnp.concatenate([before, value, after], axis=dim)
    return value


def build_columns(fields, conduct, potential):
    center = fields[:, 1:-1, 1:-1]
    k_mid = conduct[1:-1, 1:-1]
    x_plus = 0.5 * (k_mid + conduct[2:, 1:-1])
    x_minus = 0.5 * (k_mid + conduct[:-2, 1:-1])
    y_plus = 0.5 * (k_mid + conduct[1:-1, 2:])
    y_minus = 0.5 * (k_mid + conduct[1:-1, :-2])
    along_x = x_plus * (center - fields[:, 2:, 1:-1]) + x_minus * (center - fields[:, :-2, 1:-1])
    along_y = y_plus * (center - fields[:, 1:-1, 2:]) + y_minus * (center - fields[:, 1:-1, :-2])
    react = potential * center
    stacked = jnp.concatenate([center, along_x, along_y, react], 0)
    return stacked.reshape(stacked.shape[0], -1)


def inner_products(matrix, cell_count):
    return jnp.dot(matrix, matrix.T, precision=lax.Precision.HIGHEST) / cell_count


def on_device(mode_fields, conductance, potential):
    modes_count = mode_fields.shape[0]
    rows_here = mode_fields.shape[1]
    cols_here = mode_fields.shape[2]
    stacked = jnp.concatenate([mode_fields, conductance[None]], 0)
    padded = padded_2(stacked, (("gx", 1), ("gy", 2)), 1)
    matrix = build_columns(padded[:modes_count], padded[modes_count], potential)
    cell_count = float(rows_here * cols_here * lax.axis_size("gx") * lax.axis_size("gy"))
    gram_total = lax.psum(inner_products(matrix, cell_count), ("gx", "gy"))
    lower_tri = jnp.linalg.cholesky(gram_total)
    basis_flat = jax.scipy.linalg.solve_triangular(lower_tri, matrix, lower=True)
    basis_field = basis_flat.reshape(basis_flat.shape[0], rows_here, cols_here)
    return (basis_field, lower_tri.T)


def solution(mesh):
    placed = (P(None, "gx", "gy"), P("gx", "gy"), P("gx", "gy"))
    return jax.shard_map(
        on_device, mesh=mesh, in_specs=placed, out_specs=(P(None, "gx", "gy"), P()), check_vma=False
    )
```

profile of v0, /device:TPU:1, one launch (start us, length us, event | category | flops | bytes accessed | tf_op | source)
XLA Modules:
  0.0 232.6 jit_solution(10538956578714779694)
XLA Ops:
  7.2 0.0 all-reduce.2.cloned.1.call-start
  7.2 0.9 broadcast_in_dim.3
  8.1 5.0 %fusion.22 = (f32[32,64,256]{2,0,1:T(8,128)}, f32[33,64,256]{2,0,1:T(8,128)S(1)}, f32[32,64,256]{2,0,1:T(8,128)}) fusion(f32[32,64,256]{2,1,0:T(8,128)} %param.3, f32[64,256]{1,0:T(8,128)} %param.5), kind=kLoop, calls=%fused_computation.51 | loop fusion | flops 524287 | bytes 8454144 | tf_op args[0]
  13.1 0.9 dynamic-update-slice.4
  14.0 3.9 %collective-permute-start = (f32[33,1,256]{2,0,1:T(8,128)S(1)}, f32[33,1,256]{2,0,1:T(8,128)S(1)}, u32[]{:S(2)}, u32[]{:S(2)}) collective-permute-start(f32[33,1,256]{2,0,1:T(8,128)S(1)} %get-tuple-element.12), channel_id=1, source_target_pairs={{0,4},{4,8},{8,12},{12,16},{16,20},{20,24},{24,28},{1,5},{5,9},{9,... | collective-permute-start | bytes 101384 | tf_op jit(solution)/shard_map/ppermute | solution.py:14
  17.9 1.3 collective-permute-start.1
  19.2 0.0 collective-permute-done
  19.2 3.4 %collective-permute-done.1 = f32[33,1,256]{2,0,1:T(8,128)S(1)} collective-permute-done((f32[33,1,256]{2,0,1:T(8,128)S(1)}, f32[33,1,256]{2,0,1:T(8,128)S(1)}, u32[]{:S(2)}, u32[]{:S(2)}) %collective-permute-start.1) | collective-permute-done | bytes 33824 | tf_op jit(solution)/shard_map/ppermute | solution.py:15
  22.7 0.2 pad_maximum_fusion.1
  22.8 1.9 fusion.20
  24.8 1.8 copy.32
  26.6 4.0 %collective-permute-start.3 = (f32[33,66,1]{1,2,0:T(1,128)S(1)}, f32[33,66,1]{1,2,0:T(1,128)S(1)}, u32[]{:S(2)}, u32[]{:S(2)}) collective-permute-start(f32[33,66,1]{1,2,0:T(1,128)S(1)} %copy.32), channel_id=1, source_target_pairs={{1,0},{2,1},{3,2},{5,4},{6,5},{7,6},{9,8},{10,9},{11,10},{13,12},{... | collective-permute-start | bytes 26144 | tf_op jit(solution)/shard_map/ppermute | solution.py:15
  30.6 1.8 copy.31
  32.4 3.1 %collective-permute-start.2 = (f32[33,66,1]{1,2,0:T(1,128)S(1)}, f32[33,66,1]{1,2,0:T(1,128)S(1)}, u32[]{:S(2)}, u32[]{:S(2)}) collective-permute-start(f32[33,66,1]{1,2,0:T(1,128)S(1)} %copy.31), channel_id=1, source_target_pairs={{0,1},{1,2},{2,3},{4,5},{5,6},{6,7},{8,9},{9,10},{10,11},{12,13},{... | collective-permute-start | bytes 26144 | tf_op jit(solution)/shard_map/ppermute | solution.py:14
  35.4 0.0 collective-permute-done.3
  35.4 1.7 copy.34
  37.1 0.0 collective-permute-done.2
  37.1 1.7 copy.33
  38.8 0.0 copy-start
  38.8 0.0 copy-start.1
  38.8 0.0 copy-start.2
  38.8 1.5 pad_maximum_fusion.10
  40.3 0.1 fusion.16
  40.5 0.0 copy-done
  40.5 0.2 copy-done.1
  40.7 0.7 copy-done.2
  41.3 0.0 copy-start.3
  41.3 7.0 %fusion.9 = (f32[32,64,256]{2,0,1:T(8,128)}, f32[32,64,256]{2,0,1:T(8,128)}) fusion(f32[33,64,256]{2,0,1:T(8,128)S(1)} %dynamic-update-slice.4, f32[33,1,256]{2,0,1:T(8,128)S(1)} %collective-permute-done, f32[33,1,256]{2,0,1:T(8,128)S(1)} %collective-permute-done.1, f32[64,256]{1,0:T(8,128)S(1)} %get-tuple-element.19, f32[64,256]{1,0:T(8,128)S(1)} %get-tuple-element.17, ...), kind=kLoop, calls=%fused_computation.18 | loop fusion | flops 9437184 | bytes 8801296 | tf_op jit(solution)/shard_map/add | solution.py:27
  48.3 0.0 copy-done.3
  48.3 0.0 copy-start.4
  48.3 10.7 %fusion.12 = f32[128,128]{0,1:T(8,128)} fusion(f32[32,64,256]{2,0,1:T(8,128)} %get-tuple-element.16, f32[32,64,256]{2,0,1:T(8,128)} %get-tuple-element.9, f32[32,64,256]{2,0,1:T(8,128)} %get-tuple-element.8, f32[32,64,256]{2,0,1:T(8,128)S(1)} %copy-done.3), kind=kOutput, calls=%fused_computation.23 | convolution fusion | flops 3227533312 | bytes 8454144 | tf_op jit(solution)/shard_map/dot_general | solution.py:35
  59.0 0.0 all-reduce.2.cloned.1.call-update
  59.0 0.0 copy-done.4
  59.0 5.7 %pad_maximum_fusion = f32[128,64,256]{2,0,1:T(8,128)} fusion(f32[32,64,256]{2,0,1:T(8,128)} %get-tuple-element.16, f32[32,64,256]{2,0,1:T(8,128)} %get-tuple-element.9, f32[32,64,256]{2,0,1:T(8,128)} %get-tuple-element.8, f32[32,64,256]{2,0,1:T(8,128)S(1)} %copy-done.4), kind=kLoop, calls=%fused_computation | loop fusion | flops 6291456 | bytes 16777216 | tf_op jit(solution)/shard_map/concatenate | solution.py:30
  64.7 9.0 %copy.45 = f32[128,64,256]{0,2,1:T(8,128)} copy(f32[128,64,256]{2,0,1:T(8,128)} %pad_maximum_fusion) | data formatting | bytes 16777216 | tf_op jit(solution)/shard_map/concatenate | solution.py:30
  73.7 107.6 %all-reduce.2.cloned.1.call-done = f32[128,128]{0,1:T(8,128)} async-done(((f32[128,128]{0,1:T(8,128)}), f32[128,128]{0,1:T(8,128)}) %all-reduce.2.cloned.1.call-update) | async-done | bytes 65552 | tf_op jit(solution)/shard_map/psum | solution.py:46
  181.3 0.9 copy.44
  182.3 0.9 fusion.18
  183.1 11.7 %cholesky.16 = f32[128,128]{1,0:T(8,128)S(1)} custom-call(f32[128,128]{1,0:T(8,128)S(1)} %fusion.18), custom_call_target="Cholesky" | custom-call | tf_op jit(solution)/shard_map/jit(cholesky)/cholesky | solution.py:47
  194.9 0.6 compare_reduce_fusion
  195.5 0.7 fusion.19
  196.2 0.7 copy.48
  196.9 9.8 %custom-call.7 = f32[1,128,128]{1,2,0:T(8,128)S(1)} custom-call(f32[1,128,128]{2,1,0:T(8,128)S(1)} %get-tuple-element.22), custom_call_target="InvertDiagBlocksLowerTriangular" | custom-call | tf_op jit(solution)/shard_map/jit(_solve_triangular)/triangular_solve | solution.py:48
  206.7 10.7 %fusion = f32[128,64,256]{2,0,1:T(8,128)S(1)} fusion(f32[128,64,256]{0,2,1:T(8,128)} %copy.45, f32[1,128,128]{1,2,0:T(8,128)S(1)} %custom-call.7), kind=kOutput, calls=%fused_computation.1 | convolution fusion | flops 3221225472 | bytes 16842752 | tf_op jit(solution)/shard_map/jit(_solve_triangular)/triangular_solve | solution.py:48
  217.5 8.3 %copy.47 = f32[128,64,256]{2,1,0:T(8,128)} copy(f32[128,64,256]{2,0,1:T(8,128)S(1)} %fusion) | data formatting | bytes 16777216
  (3 shorter events, 0.1 us)
Async XLA Ops:
  7.2 174.2 %all-reduce.2.cloned.1.call-start = ((), (), s32[]{:S(2)}) async-start(), calls=%async_computation | async-start | bytes 131072 | tf_op jit(solution)/shard_map/psum | solution.py:46
  14.0 5.2 %collective-permute-start = (f32[33,1,256]{2,0,1:T(8,128)S(1)}, f32[33,1,256]{2,0,1:T(8,128)S(1)}, u32[]{:S(2)}, u32[]{:S(2)}) collective-permute-start(f32[33,1,256]{2,0,1:T(8,128)S(1)} %get-tuple-element.12), channel_id=1, source_target_pairs={{0,4},{4,8},{8,12},{12,16},{16,20},{20,24},{24,28},{1,5},{5,9},{9,... | collective-permute-start | bytes 101384 | tf_op jit(solution)/shard_map/ppermute | solution.py:14
  17.9 4.7 %collective-permute-start.1 = (f32[33,1,256]{2,0,1:T(8,128)S(1)}, f32[33,1,256]{2,0,1:T(8,128)S(1)}, u32[]{:S(2)}, u32[]{:S(2)}) collective-permute-start(f32[33,1,256]{2,0,1:T(8,128)S(1)} %get-tuple-element.13), channel_id=1, source_target_pairs={{4,0},{8,4},{12,8},{16,12},{20,16},{24,20},{28,24},{5,1},{9,5},{13... | collective-permute-start | bytes 101384 | tf_op jit(solution)/shard_map/ppermute | solution.py:15
  26.6 8.9 %collective-permute-start.3 = (f32[33,66,1]{1,2,0:T(1,128)S(1)}, f32[33,66,1]{1,2,0:T(1,128)S(1)}, u32[]{:S(2)}, u32[]{:S(2)}) collective-permute-start(f32[33,66,1]{1,2,0:T(1,128)S(1)} %copy.32), channel_id=1, source_target_pairs={{1,0},{2,1},{3,2},{5,4},{6,5},{7,6},{9,8},{10,9},{11,10},{13,12},{... | collective-permute-start | bytes 26144 | tf_op jit(solution)/shard_map/ppermute | solution.py:15
  32.4 4.7 %collective-permute-start.2 = (f32[33,66,1]{1,2,0:T(1,128)S(1)}, f32[33,66,1]{1,2,0:T(1,128)S(1)}, u32[]{:S(2)}, u32[]{:S(2)}) collective-permute-start(f32[33,66,1]{1,2,0:T(1,128)S(1)} %copy.31), channel_id=1, source_target_pairs={{0,1},{1,2},{2,3},{4,5},{5,6},{6,7},{8,9},{9,10},{10,11},{12,13},{... | collective-permute-start | bytes 26144 | tf_op jit(solution)/shard_map/ppermute | solution.py:14
  38.8 1.7 copy-start
  38.8 1.9 copy-start.1
  38.8 2.6 %copy-start.2 = (f32[32,64,256]{2,1,0:T(8,128)S(1)}, f32[32,64,256]{2,1,0:T(8,128)}, u32[]{:S(2)}) copy-start(f32[32,64,256]{2,1,0:T(8,128)} %param.3) | copy-start | bytes 6291460
  41.3 7.0 %copy-start.3 = (f32[32,64,256]{2,0,1:T(8,128)S(1)}, f32[32,64,256]{2,0,1:T(8,128)}, u32[]{:S(2)}) copy-start(f32[32,64,256]{2,0,1:T(8,128)} %get-tuple-element.14) | copy-start | bytes 6291460
  48.3 10.7 %copy-start.4 = (f32[32,64,256]{2,0,1:T(8,128)S(1)}, f32[32,64,256]{2,0,1:T(8,128)}, u32[]{:S(2)}) copy-start(f32[32,64,256]{2,0,1:T(8,128)} %get-tuple-element.14) | copy-start | bytes 6291460
Sparse Core Ops, SparseCore 0:
  59.2 122.1 all-reduce.1
where the time goes:
time: 233 us
  waiting for transfers between devices  111 us (48%)
  other arithmetic  43.2 us (19%)
  local copies, waits for them, and re-layouts  30.4 us (13%)
  matrix products  21.4 us (9%)
  between operations  14.2 us (6%)
  starting transfers between devices  12.3 us (5%)
    psum x1, waiting for transfers between devices, on_device(): gram_total = lax.psum(inner_products(matrix, cell_count), ('gx', 'gy'))  108 us
    another operation x3, other arithmetic, on_device(): lower_tri = jnp.linalg.cholesky(gram_total)  12.4 us
    another operation x1, matrix products, on_device(): jax.scipy.linalg.solve_triangular(lower_tri, matrix, lower=True)  10.7 us
    dot_general x1, matrix products, inner_products(): jnp.dot(matrix, matrix.T, precision=lax.Precision.HIGHEST) / cell_count  10.7 us
    unnamed x13, local copies, waits for them, and re-layouts  9.88 us
    another operation x1, other arithmetic, on_device(): jax.scipy.linalg.solve_triangular(lower_tri, matrix, lower=True)  9.81 us
    concatenate x1, local copies, waits for them, and re-layouts, build_columns(): stacked = jnp.concatenate([center, along_x, along_y, react], 0)  9.01 us
    ppermute x2, starting transfers between devices, padded_2(): before = lax.ppermute(last, axis, up)  6.99 us
  transfers between devices with their start and end apart: 5, of which 2 were waited for; matrix products, arithmetic and copies ran while one was open for 8% of the time, Pallas kernels for 0%

commit v1 on v0

--- a/solution.py
+++ b/solution.py
@@ -43,7 +43,7 @@
     padded = padded_2(stacked, (("gx", 1), ("gy", 2)), 1)
     matrix = build_columns(padded[:modes_count], padded[modes_count], potential)
     cell_count = float(rows_here * cols_here * lax.axis_size("gx") * lax.axis_size("gy"))
-    gram_total = lax.psum(inner_products(matrix, cell_count), ("gx", "gy"))
+    gram_total = lax.psum(lax.psum(inner_products(matrix, cell_count), "gy"), "gx")
     lower_tri = jnp.linalg.cholesky(gram_total)
     basis_flat = jax.scipy.linalg.solve_triangular(lower_tri, matrix, lower=True)
     basis_field = basis_flat.reshape(basis_flat.shape[0], rows_here, cols_here)

time: 233 us -> 217 us (0.931); the launches traced: 233 us -> 214 us
  waiting for transfers between devices: 111 us -> 91.9 us
    psum x1 -> x2, waiting for transfers between devices: 108 us -> 88.4 us  [the longest x1 57.6 us: on_device(): lax.psum(lax.psum(inner_products(matrix, cell_count), 'gy'), 'gx')]
  transfers between devices with their start and end apart: 5 -> 6, of which waited for: 2 -> 3; matrix products, arithmetic and copies ran while one was open for 8% -> 8% of each run, Pallas kernels for 0% -> 0%
where the time goes in v1:
time: 217 us; the launch traced here: 214 us
  waiting for transfers between devices  91.9 us (42%)
  other arithmetic  43.2 us (20%)
  local copies, waits for them, and re-layouts  30.4 us (14%)
  matrix products  21.4 us (10%)
  between operations  14.2 us (7%)
  starting transfers between devices  12.6 us (6%)
    psum x1, waiting for transfers between devices, on_device(): lax.psum(lax.psum(inner_products(matrix, cell_count), 'gy'), 'gx')  57.6 us
    psum x1, waiting for transfers between devices, on_device(): lax.psum(inner_products(matrix, cell_count), 'gy')  30.9 us
    another operation x3, other arithmetic, on_device(): lower_tri = jnp.linalg.cholesky(gram_total)  12.4 us
    another operation x1, matrix products, on_device(): jax.scipy.linalg.solve_triangular(lower_tri, matrix, lower=True)  10.7 us
    dot_general x1, matrix products, inner_products(): jnp.dot(matrix, matrix.T, precision=lax.Precision.HIGHEST) / cell_count  10.7 us
    unnamed x13, local copies, waits for them, and re-layouts  9.88 us
    another operation x1, other arithmetic, on_device(): jax.scipy.linalg.solve_triangular(lower_tri, matrix, lower=True)  9.81 us
    concatenate x1, local copies, waits for them, and re-layouts, build_columns(): stacked = jnp.concatenate([center, along_x, along_y, react], 0)  9.01 us
  transfers between devices with their start and end apart: 6, of which 3 were waited for; matrix products, arithmetic and copies ran while one was open for 8% of the time, Pallas kernels for 0%

profile of v1, /device:TPU:1, one launch (start us, length us, event | category | flops | bytes accessed | tf_op | source)
XLA Modules:
  0.0 213.7 jit_solution(12785266310437195147)
XLA Ops:
  7.2 0.0 all-reduce.3.cloned.1.call-start
  7.2 0.9 broadcast_in_dim.3
  8.1 5.0 %fusion.22 = (f32[32,64,256]{2,0,1:T(8,128)}, f32[33,64,256]{2,0,1:T(8,128)S(1)}, f32[32,64,256]{2,0,1:T(8,128)}) fusion(f32[32,64,256]{2,1,0:T(8,128)} %param.3, f32[64,256]{1,0:T(8,128)} %param.5), kind=kLoop, calls=%fused_computation.51 | loop fusion | flops 524287 | bytes 8454144 | tf_op args[0]
  13.1 0.9 dynamic-update-slice.4
  14.0 3.9 %collective-permute-start = (f32[33,1,256]{2,0,1:T(8,128)S(1)}, f32[33,1,256]{2,0,1:T(8,128)S(1)}, u32[]{:S(2)}, u32[]{:S(2)}) collective-permute-start(f32[33,1,256]{2,0,1:T(8,128)S(1)} %get-tuple-element.12), channel_id=1, source_target_pairs={{0,4},{4,8},{8,12},{12,16},{16,20},{20,24},{24,28},{1,5},{5,9},{9,... | collective-permute-start | bytes 101384 | tf_op jit(solution)/shard_map/ppermute | solution.py:14
  17.9 1.3 collective-permute-start.1
  19.2 0.0 collective-permute-done
  19.2 3.4 %collective-permute-done.1 = f32[33,1,256]{2,0,1:T(8,128)S(1)} collective-permute-done((f32[33,1,256]{2,0,1:T(8,128)S(1)}, f32[33,1,256]{2,0,1:T(8,128)S(1)}, u32[]{:S(2)}, u32[]{:S(2)}) %collective-permute-start.1) | collective-permute-done | bytes 33824 | tf_op jit(solution)/shard_map/ppermute | solution.py:15
  22.7 0.2 pad_maximum_fusion.1
  22.8 1.9 fusion.20
  24.8 1.8 copy.32
  26.6 4.0 %collective-permute-start.3 = (f32[33,66,1]{1,2,0:T(1,128)S(1)}, f32[33,66,1]{1,2,0:T(1,128)S(1)}, u32[]{:S(2)}, u32[]{:S(2)}) collective-permute-start(f32[33,66,1]{1,2,0:T(1,128)S(1)} %copy.32), channel_id=1, source_target_pairs={{1,0},{2,1},{3,2},{5,4},{6,5},{7,6},{9,8},{10,9},{11,10},{13,12},{... | collective-permute-start | bytes 26144 | tf_op jit(solution)/shard_map/ppermute | solution.py:15
  30.6 1.8 copy.31
  32.4 3.1 %collective-permute-start.2 = (f32[33,66,1]{1,2,0:T(1,128)S(1)}, f32[33,66,1]{1,2,0:T(1,128)S(1)}, u32[]{:S(2)}, u32[]{:S(2)}) collective-permute-start(f32[33,66,1]{1,2,0:T(1,128)S(1)} %copy.31), channel_id=1, source_target_pairs={{0,1},{1,2},{2,3},{4,5},{5,6},{6,7},{8,9},{9,10},{10,11},{12,13},{... | collective-permute-start | bytes 26144 | tf_op jit(solution)/shard_map/ppermute | solution.py:14
  35.4 0.0 collective-permute-done.3
  35.4 1.7 copy.34
  37.1 0.0 collective-permute-done.2
  37.1 1.7 copy.33
  38.8 0.0 copy-start
  38.8 0.0 copy-start.1
  38.8 0.0 copy-start.2
  38.8 1.5 pad_maximum_fusion.10
  40.3 0.1 fusion.16
  40.5 0.0 copy-done
  40.5 0.2 copy-done.1
  40.7 0.7 copy-done.2
  41.3 0.0 copy-start.3
  41.3 7.0 %fusion.9 = (f32[32,64,256]{2,0,1:T(8,128)}, f32[32,64,256]{2,0,1:T(8,128)}) fusion(f32[33,64,256]{2,0,1:T(8,128)S(1)} %dynamic-update-slice.4, f32[33,1,256]{2,0,1:T(8,128)S(1)} %collective-permute-done, f32[33,1,256]{2,0,1:T(8,128)S(1)} %collective-permute-done.1, f32[64,256]{1,0:T(8,128)S(1)} %get-tuple-element.19, f32[64,256]{1,0:T(8,128)S(1)} %get-tuple-element.17, ...), kind=kLoop, calls=%fused_computation.18 | loop fusion | flops 9437184 | bytes 8801296 | tf_op jit(solution)/shard_map/add | solution.py:27
  48.3 0.0 copy-done.3
  48.3 0.0 copy-start.4
  48.3 10.7 %fusion.12 = f32[128,128]{0,1:T(8,128)} fusion(f32[32,64,256]{2,0,1:T(8,128)} %get-tuple-element.16, f32[32,64,256]{2,0,1:T(8,128)} %get-tuple-element.9, f32[32,64,256]{2,0,1:T(8,128)} %get-tuple-element.8, f32[32,64,256]{2,0,1:T(8,128)S(1)} %copy-done.3), kind=kOutput, calls=%fused_computation.23 | convolution fusion | flops 3227533312 | bytes 8454144 | tf_op jit(solution)/shard_map/dot_general | solution.py:35
  59.0 0.0 all-reduce.3.cloned.1.call-update
  59.0 0.2 all-reduce.5.cloned.1.call-start
  59.3 30.9 %all-reduce.3.cloned.1.call-done = f32[128,128]{0,1:T(8,128)} async-done(((f32[128,128]{0,1:T(8,128)}), f32[128,128]{0,1:T(8,128)}) %all-reduce.3.cloned.1.call-update) | async-done | bytes 65552 | tf_op jit(solution)/shard_map/psum | solution.py:46
  90.1 0.0 all-reduce.5.cloned.1.call-update
  90.2 0.0 copy-done.4
  90.2 5.7 %pad_maximum_fusion = f32[128,64,256]{2,0,1:T(8,128)} fusion(f32[32,64,256]{2,0,1:T(8,128)} %get-tuple-element.16, f32[32,64,256]{2,0,1:T(8,128)} %get-tuple-element.9, f32[32,64,256]{2,0,1:T(8,128)} %get-tuple-element.8, f32[32,64,256]{2,0,1:T(8,128)S(1)} %copy-done.4), kind=kLoop, calls=%fused_computation | loop fusion | flops 6291456 | bytes 16777216 | tf_op jit(solution)/shard_map/concatenate | solution.py:30
  95.9 9.0 %copy.45 = f32[128,64,256]{0,2,1:T(8,128)} copy(f32[128,64,256]{2,0,1:T(8,128)} %pad_maximum_fusion) | data formatting | bytes 16777216 | tf_op jit(solution)/shard_map/concatenate | solution.py:30
  104.9 57.6 %all-reduce.5.cloned.1.call-done = f32[128,128]{0,1:T(8,128)} async-done(((f32[128,128]{0,1:T(8,128)}), f32[128,128]{0,1:T(8,128)}) %all-reduce.5.cloned.1.call-update) | async-done | bytes 65552 | tf_op jit(solution)/shard_map/psum | solution.py:46
  162.4 0.9 copy.44
  163.4 0.9 fusion.18
  164.2 11.7 %cholesky.16 = f32[128,128]{1,0:T(8,128)S(1)} custom-call(f32[128,128]{1,0:T(8,128)S(1)} %fusion.18), custom_call_target="Cholesky" | custom-call | tf_op jit(solution)/shard_map/jit(cholesky)/cholesky | solution.py:47
  176.0 0.6 compare_reduce_fusion
  176.6 0.7 fusion.19
  177.3 0.7 copy.48
  178.0 9.8 %custom-call.7 = f32[1,128,128]{1,2,0:T(8,128)S(1)} custom-call(f32[1,128,128]{2,1,0:T(8,128)S(1)} %get-tuple-element.22), custom_call_target="InvertDiagBlocksLowerTriangular" | custom-call | tf_op jit(solution)/shard_map/jit(_solve_triangular)/triangular_solve | solution.py:48
  187.8 10.7 %fusion = f32[128,64,256]{2,0,1:T(8,128)S(1)} fusion(f32[128,64,256]{0,2,1:T(8,128)} %copy.45, f32[1,128,128]{1,2,0:T(8,128)S(1)} %custom-call.7), kind=kOutput, calls=%fused_computation.1 | convolution fusion | flops 3221225472 | bytes 16842752 | tf_op jit(solution)/shard_map/jit(_solve_triangular)/triangular_solve | solution.py:48
  198.6 8.3 %copy.47 = f32[128,64,256]{2,1,0:T(8,128)} copy(f32[128,64,256]{2,0,1:T(8,128)S(1)} %fusion) | data formatting | bytes 16777216
  (3 shorter events, 0.1 us)
Async XLA Ops:
  7.2 83.0 %all-reduce.3.cloned.1.call-start = ((), (), s32[]{:S(2)}) async-start(), calls=%async_computation | async-start | bytes 131072 | tf_op jit(solution)/shard_map/psum | solution.py:46
  14.0 5.2 %collective-permute-start = (f32[33,1,256]{2,0,1:T(8,128)S(1)}, f32[33,1,256]{2,0,1:T(8,128)S(1)}, u32[]{:S(2)}, u32[]{:S(2)}) collective-permute-start(f32[33,1,256]{2,0,1:T(8,128)S(1)} %get-tuple-element.12), channel_id=1, source_target_pairs={{0,4},{4,8},{8,12},{12,16},{16,20},{20,24},{24,28},{1,5},{5,9},{9,... | collective-permute-start | bytes 101384 | tf_op jit(solution)/shard_map/ppermute | solution.py:14
  17.9 4.7 %collective-permute-start.1 = (f32[33,1,256]{2,0,1:T(8,128)S(1)}, f32[33,1,256]{2,0,1:T(8,128)S(1)}, u32[]{:S(2)}, u32[]{:S(2)}) collective-permute-start(f32[33,1,256]{2,0,1:T(8,128)S(1)} %get-tuple-element.13), channel_id=1, source_target_pairs={{4,0},{8,4},{12,8},{16,12},{20,16},{24,20},{28,24},{5,1},{9,5},{13... | collective-permute-start | bytes 101384 | tf_op jit(solution)/shard_map/ppermute | solution.py:15
  26.6 8.9 %collective-permute-start.3 = (f32[33,66,1]{1,2,0:T(1,128)S(1)}, f32[33,66,1]{1,2,0:T(1,128)S(1)}, u32[]{:S(2)}, u32[]{:S(2)}) collective-permute-start(f32[33,66,1]{1,2,0:T(1,128)S(1)} %copy.32), channel_id=1, source_target_pairs={{1,0},{2,1},{3,2},{5,4},{6,5},{7,6},{9,8},{10,9},{11,10},{13,12},{... | collective-permute-start | bytes 26144 | tf_op jit(solution)/shard_map/ppermute | solution.py:15
  32.4 4.7 %collective-permute-start.2 = (f32[33,66,1]{1,2,0:T(1,128)S(1)}, f32[33,66,1]{1,2,0:T(1,128)S(1)}, u32[]{:S(2)}, u32[]{:S(2)}) collective-permute-start(f32[33,66,1]{1,2,0:T(1,128)S(1)} %copy.31), channel_id=1, source_target_pairs={{0,1},{1,2},{2,3},{4,5},{5,6},{6,7},{8,9},{9,10},{10,11},{12,13},{... | collective-permute-start | bytes 26144 | tf_op jit(solution)/shard_map/ppermute | solution.py:14
  38.8 1.7 copy-start
  38.8 1.9 copy-start.1
  38.8 2.6 %copy-start.2 = (f32[32,64,256]{2,1,0:T(8,128)S(1)}, f32[32,64,256]{2,1,0:T(8,128)}, u32[]{:S(2)}) copy-start(f32[32,64,256]{2,1,0:T(8,128)} %param.3) | copy-start | bytes 6291460
  41.3 7.0 %copy-start.3 = (f32[32,64,256]{2,0,1:T(8,128)S(1)}, f32[32,64,256]{2,0,1:T(8,128)}, u32[]{:S(2)}) copy-start(f32[32,64,256]{2,0,1:T(8,128)} %get-tuple-element.14) | copy-start | bytes 6291460
  48.3 41.8 %copy-start.4 = (f32[32,64,256]{2,0,1:T(8,128)S(1)}, f32[32,64,256]{2,0,1:T(8,128)}, u32[]{:S(2)}) copy-start(f32[32,64,256]{2,0,1:T(8,128)} %get-tuple-element.14) | copy-start | bytes 6291460
  59.0 103.4 %all-reduce.5.cloned.1.call-start = ((), (), s32[]{:S(2)}) async-start(), calls=%async_computation.1 | async-start | bytes 131072 | tf_op jit(solution)/shard_map/psum | solution.py:46
Sparse Core Ops, SparseCore 0:
  59.2 30.9 all-reduce.2
  93.5 68.8 all-reduce.4
